TPU v7x, 32 devices: a whole 2x2x4 slice. The times are simulated.
32 devices in a mesh: dp: 2 (over x), lat: 4 (over y, core), lon: 4 (over z).
Axes of the slice: x: 2, y: 2, z: 4, core: 2. Of those that a mesh axis runs over, the one named last changes fastest.
Arguments:
- hidden_in: bfloat16 [2, 64, 512, 128], P('dp', 'lat', 'lon'), may hold values from -6 to 6
- conv_weight: bfloat16 [3, 3, 128, 128], replicated, may hold values from -0.1875 to 0.1875
- conv_bias: float32 [128], replicated, may hold values from -3 to 3
- proj_weight: float32 [128], replicated, may hold values from -5 to 5
- ocean_depth: float32 [64, 512], P('lat', 'lon'), may hold values from 0.5 to 2
- sea_mask: int32 [64, 512], P('lat', 'lon'), may hold values 0 or 1
- step_alpha: float32 [6], replicated, may hold values from 0.04 to 0.07
- step_beta: float32 [6], replicated, may hold values from 0.1 to 0.5
- surface_cotangent: float32 [2, 64, 512], P('dp', 'lat', 'lon'), may hold values from -20 to 20
Outputs:
- grad_hidden: bfloat16 [2, 64, 512, 128], P('dp', 'lat', 'lon')
- grad_weight: float32 [128, 3, 3, 128], P(('lat', 'lon'))
- grad_bias: float32 [128], replicated
- grad_proj: float32 [128], replicated
All inputs are finite; a program needn't handle non-finite values. No bound on the sum of `sea_mask` on one device may be relied on, other than what follows from the above.
Results may differ from a plain program's by a relative error of at most 0.01.
Values may be sent and summed in bfloat16 or wider, within the bound.
A program may use at most 64 MiB of HBM per device.

v0:
```python
import math

import jax
import jax.numpy as jnp
from jax import lax
from jax.sharding import PartitionSpec as P

ITERS = 6


helm_coef = 0.5


def extended(cells, sides, width, closed):
    for axis, dim in sides:
        count = lax.axis_size(axis)
        ends = count if closed else count - 1
        head = lax.slice_in_dim(cells, 0, width, axis=dim)
        tail = lax.slice_in_dim(cells, cells.shape[dim] - width, cells.shape[dim], axis=dim)
        cells = jnp.concatenate(
            [
                lax.ppermute(tail, axis, [(i, (i + 1) % count) for i in range(ends)]),
                cells,
                lax.ppermute(head, axis, [((i + 1) % count, i) for i in range(ends)]),
            ],
            axis=dim,
        )
    return cells


def operate(field_ext, mask_ext, depth_ext):
    rows_in = field_ext.shape[-2] - 2
    cols_in = field_ext.shape[-1] - 2
    center = field_ext[..., 1:-1, 1:-1]
    mask_mid = mask_ext[1:-1, 1:-1]
    depth_mid = depth_ext[1:-1, 1:-1]
    result = helm_coef * center
    for row_off, col_off in ((0, 1), (2, 1), (1, 0), (1, 2)):
        beside = field_ext[..., row_off : row_off + rows_in, col_off : col_off + cols_in]
        mask_near = mask_ext[row_off : row_off + rows_in, col_off : col_off + cols_in]
        depth_near = depth_ext[row_off : row_off + rows_in, col_off : col_off + cols_in]
        weight = mask_near * 0.5 * (depth_mid + depth_near)
        result = result + weight * (center - beside)
    return mask_mid * result


def solve_steps(adjoint_start, mask_ext, depth_ext, step_alpha, step_beta, widen):
    solution = jnp.zeros_like(adjoint_start)
    residual = adjoint_start
    direction = adjoint_start
    for turn_index in range(ITERS):
        solution = solution + step_alpha[turn_index] * direction
        if turn_index + 1 < ITERS:
            applied = operate(widen(direction), mask_ext, depth_ext)
            residual = residual - step_alpha[turn_index] * applied
            direction = residual + step_beta[turn_index] * direction
    return solution


def halo_field(field):
    field = extended(field, (("lat", 1),), 1, False)
    return extended(field, (("lon", 2),), 1, True)


def shards(
    hidden_in,
    conv_weight,
    conv_bias,
    proj_weight,
    ocean_depth,
    sea_mask,
    step_alpha,
    step_beta,
    surface_cotangent,
):
    samples, lat_rows, lon_cols, channels = hidden_in.shape
    mask_float = sea_mask.astype(jnp.float32)
    counted, summed = lax.psum(
        (jnp.sum(mask_float), jnp.sum(mask_float * surface_cotangent, axis=(1, 2))), ("lat", "lon")
    )
    adjoint_start = mask_float * (surface_cotangent - (summed / counted)[:, None, None])
    coefs = jnp.stack([mask_float, ocean_depth])
    coefs = extended(coefs, (("lat", 1),), 1, False)
    coefs = extended(coefs, (("lon", 2),), 1, True)
    solution = solve_steps(adjoint_start, coefs[0], coefs[1], step_alpha, step_beta, halo_field)
    forcing_grad = mask_float * solution
    padded = extended(hidden_in, (("lat", 1),), 1, False)
    padded = extended(padded, (("lon", 2),), 1, True)
    cell_count = samples * lat_rows * lon_cols
    shifted = [
        padded[:, row_off : row_off + lat_rows, col_off : col_off + lon_cols, :].reshape(
            cell_count, channels
        )
        for row_off in range(3)
        for col_off in range(3)
    ]
    preact = conv_bias
    for offset in range(9):
        preact = preact + jnp.dot(
            shifted[offset],
            conv_weight[offset // 3, offset % 3],
            preferred_element_type=jnp.float32,
        )
    sigma = jax.nn.sigmoid(preact)
    active = preact * sigma
    slope_act = sigma * (1.0 + preact * (1.0 - sigma))
    force_col = forcing_grad.reshape(cell_count)[:, None]
    grad_pre = (force_col * proj_weight * slope_act).astype(jnp.bfloat16)
    local_proj = jnp.sum(active * force_col, axis=0)
    local_bias = jnp.sum(grad_pre.astype(jnp.float32), axis=0)
    grad_ext = extended(
        grad_pre.reshape(samples, lat_rows, lon_cols, channels), (("lat", 1),), 1, False
    )
    grad_ext = extended(grad_ext, (("lon", 2),), 1, True)
    backed = jnp.zeros((cell_count, channels), jnp.float32)
    for row_off in range(3):
        for col_off in range(3):
            window = grad_ext[
                :, 2 - row_off : 2 - row_off + lat_rows, 2 - col_off : 2 - col_off + lon_cols, :
            ].reshape(cell_count, channels)
            backed = backed + lax.dot_general(
                window,
                conv_weight[row_off, col_off],
                (((1,), (1,)), ((), ())),
                preferred_element_type=jnp.float32,
            )
    grad_hidden = backed.reshape(samples, lat_rows, lon_cols, channels).astype(jnp.bfloat16)
    share = channels // lax.axis_size(("lat", "lon"))
    blocks = []
    for shifted_cols in shifted:
        blocks.append(
            lax.dot_general(
                shifted_cols, grad_pre, (((0,), (0,)), ((), ())), preferred_element_type=jnp.float32
            )
        )
    spatial = lax.psum_scatter(
        jnp.stack(blocks, axis=1).reshape(share * lax.axis_size(("lat", "lon")), 3, 3, channels),
        ("lat", "lon"),
        scatter_dimension=0,
        tiled=True,
    )
    own_weight = lax.psum(spatial, "dp")
    total_bias, total_proj = lax.psum((local_bias, local_proj), ("dp", "lat", "lon"))
    all_cells = cell_count * lax.axis_size("dp") * lax.axis_size("lat") * lax.axis_size("lon")
    grad_scale = 1.0 / math.sqrt(all_cells)
    return (grad_hidden, own_weight * grad_scale, total_bias * grad_scale, total_proj * grad_scale)


def solution(mesh):
    in_specs = (
        P("dp", "lat", "lon", None),
        P(),
        P(),
        P(),
        P("lat", "lon"),
        P("lat", "lon"),
        P(),
        P(),
        P("dp", "lat", "lon"),
    )
    out_specs = (P("dp", "lat", "lon", None), P(("lat", "lon"), None, None, None), P(), P())
    return jax.shard_map(shards, mesh=mesh, in_specs=in_specs, out_specs=out_specs, check_vma=False)
```

profile of v0, /device:TPU:0, one launch (start us, length us, event | category | flops | bytes accessed | tf_op | source)
XLA Modules:
  0.0 225.2 jit_solution(6670252528962750081)
XLA Ops:
  8.7 2.4 %collective-permute-start = (f32[2,1,128]{2,1,0:T(1,128)S(1)}, f32[2,1,128]{2,1,0:T(1,128)S(1)}, u32[]{:S(2)}, u32[]{:S(2)}) collective-permute-start(f32[2,1,128]{2,1,0:T(1,128)S(1)} %get-tuple-element.57), channel_id=1, source_target_pairs={{0,4},{4,8},{8,12},{1,5},{5,9},{9,13},{2,6},{6,10},{10,14},{3,7},{... | collective-permute-start | bytes 3080 | tf_op jit(solution)/shard_map/ppermute | solution.py:22
  15.0 36.6 %all-reduce.1 = (f32[1]{0:T(128)}, f32[1]{0:T(128)}) all-reduce(f32[1]{0:T(128)} %bitcast.2, f32[1]{0:T(128)} %bitcast.3), channel_id=1, replica_groups=mesh['dp'=2,'lat'=4,'lon'=4] {'lat','lon'}, use_global_device_ids=true, to_apply=%region_1.0 | all-reduce | flops 2 | bytes 16 | tf_op jit(solution)/shard_map/psum | solution.py:78
  61.0 3.7 %collective-permute-start.3 = (f32[2,18,1]{2,1,0:T(8,128)S(1)}, f32[2,18,1]{2,1,0:T(8,128)S(1)}, u32[]{:S(2)}, u32[]{:S(2)}) collective-permute-start(f32[2,18,1]{2,1,0:T(8,128)S(1)} %get-tuple-element.56), channel_id=1, source_target_pairs={{1,0},{2,1},{3,2},{0,3},{5,4},{6,5},{7,6},{4,7},{9,8},{10,9},{11,1... | collective-permute-start | bytes 440 | tf_op jit(solution)/shard_map/ppermute | solution.py:24
  64.7 2.0 collective-permute-start.7
  69.7 2.6 %collective-permute-start.8 = (f32[1,1,128]{2,1,0:T(1,128)S(1)}, f32[1,1,128]{2,1,0:T(1,128)S(1)}, u32[]{:S(2)}, u32[]{:S(2)}) collective-permute-start(f32[1,1,128]{2,1,0:T(1,128)S(1)} %get-tuple-element.75), channel_id=1, source_target_pairs={{0,4},{4,8},{8,12},{1,5},{5,9},{9,13},{2,6},{6,10},{10,14},{3,7},{... | collective-permute-start | bytes 1544 | tf_op jit(solution)/shard_map/ppermute | solution.py:22
  73.6 4.7 %collective-permute-done.9 = f32[1,1,128]{2,1,0:T(1,128)S(1)} collective-permute-done((f32[1,1,128]{2,1,0:T(1,128)S(1)}, f32[1,1,128]{2,1,0:T(1,128)S(1)}, u32[]{:S(2)}, u32[]{:S(2)}) %collective-permute-start.9) | collective-permute-done | bytes 544 | tf_op jit(solution)/shard_map/ppermute | solution.py:24
  78.4 3.8 %collective-permute-start.11 = (f32[1,18,1]{2,1,0:T(8,128)S(1)}, f32[1,18,1]{2,1,0:T(8,128)S(1)}, u32[]{:S(2)}, u32[]{:S(2)}) collective-permute-start(f32[1,18,1]{2,1,0:T(8,128)S(1)} %get-tuple-element.66), channel_id=1, source_target_pairs={{1,0},{2,1},{3,2},{0,3},{5,4},{6,5},{7,6},{4,7},{9,8},{10,9},{11,1... | collective-permute-start | bytes 224 | tf_op jit(solution)/shard_map/ppermute | solution.py:24
  82.2 1.7 collective-permute-done.10
  85.2 3.3 %collective-permute-start.12 = (f32[1,1,128]{2,1,0:T(1,128)S(1)}, f32[1,1,128]{2,1,0:T(1,128)S(1)}, u32[]{:S(2)}, u32[]{:S(2)}) collective-permute-start(f32[1,1,128]{2,1,0:T(1,128)S(1)} %get-tuple-element.73), channel_id=1, source_target_pairs={{0,4},{4,8},{8,12},{1,5},{5,9},{9,13},{2,6},{6,10},{10,14},{3,7},{... | collective-permute-start | bytes 1544 | tf_op jit(solution)/shard_map/ppermute | solution.py:22
  89.9 2.2 collective-permute-done.13
  93.3 2.8 %collective-permute-start.15 = (f32[1,18,1]{2,1,0:T(8,128)S(1)}, f32[1,18,1]{2,1,0:T(8,128)S(1)}, u32[]{:S(2)}, u32[]{:S(2)}) collective-permute-start(f32[1,18,1]{2,1,0:T(8,128)S(1)} %get-tuple-element.64), channel_id=1, source_target_pairs={{1,0},{2,1},{3,2},{0,3},{5,4},{6,5},{7,6},{4,7},{9,8},{10,9},{11,1... | collective-permute-start | bytes 224 | tf_op jit(solution)/shard_map/ppermute | solution.py:24
  99.0 3.4 %collective-permute-start.16 = (f32[1,1,128]{2,1,0:T(1,128)S(1)}, f32[1,1,128]{2,1,0:T(1,128)S(1)}, u32[]{:S(2)}, u32[]{:S(2)}) collective-permute-start(f32[1,1,128]{2,1,0:T(1,128)S(1)} %get-tuple-element.71), channel_id=1, source_target_pairs={{0,4},{4,8},{8,12},{1,5},{5,9},{9,13},{2,6},{6,10},{10,14},{3,7},{... | collective-permute-start | bytes 1544 | tf_op jit(solution)/shard_map/ppermute | solution.py:22
  103.7 2.2 collective-permute-done.17
  107.3 2.6 %collective-permute-start.19 = (f32[1,18,1]{2,1,0:T(8,128)S(1)}, f32[1,18,1]{2,1,0:T(8,128)S(1)}, u32[]{:S(2)}, u32[]{:S(2)}) collective-permute-start(f32[1,18,1]{2,1,0:T(8,128)S(1)} %get-tuple-element.62), channel_id=1, source_target_pairs={{1,0},{2,1},{3,2},{0,3},{5,4},{6,5},{7,6},{4,7},{9,8},{10,9},{11,1... | collective-permute-start | bytes 224 | tf_op jit(solution)/shard_map/ppermute | solution.py:24
  112.8 3.4 %collective-permute-start.20 = (f32[1,1,128]{2,1,0:T(1,128)S(1)}, f32[1,1,128]{2,1,0:T(1,128)S(1)}, u32[]{:S(2)}, u32[]{:S(2)}) collective-permute-start(f32[1,1,128]{2,1,0:T(1,128)S(1)} %get-tuple-element.69), channel_id=1, source_target_pairs={{0,4},{4,8},{8,12},{1,5},{5,9},{9,13},{2,6},{6,10},{10,14},{3,7},{... | collective-permute-start | bytes 1544 | tf_op jit(solution)/shard_map/ppermute | solution.py:22
  117.5 3.5 %collective-permute-start.24 = (bf16[1,1,128,128]{3,2,1,0:T(8,128)(2,1)S(1)}, bf16[1,1,128,128]{3,2,1,0:T(8,128)(2,1)S(1)}, u32[]{:S(2)}, u32[]{:S(2)}) collective-permute-start(bf16[1,1,128,128]{3,2,1,0:T(8,128)(2,1)S(1)} %get-tuple-element.52), channel_id=1, source_target_pairs={{0,4},{4,8},{8,12},{1,5},{5,9},{9,13},{2,6},{6,10},{10,14},{3,7},{... | collective-permute-start | bytes 98312 | tf_op jit(solution)/shard_map/ppermute | solution.py:22
  123.7 2.6 %collective-permute-start.23 = (f32[1,18,1]{2,1,0:T(8,128)S(1)}, f32[1,18,1]{2,1,0:T(8,128)S(1)}, u32[]{:S(2)}, u32[]{:S(2)}) collective-permute-start(f32[1,18,1]{2,1,0:T(8,128)S(1)} %get-tuple-element.60), channel_id=1, source_target_pairs={{1,0},{2,1},{3,2},{0,3},{5,4},{6,5},{7,6},{4,7},{9,8},{10,9},{11,1... | collective-permute-start | bytes 224 | tf_op jit(solution)/shard_map/ppermute | solution.py:24
  128.0 4.5 %fusion.69 = f32[2048]{0:T(1024)S(1)} fusion(f32[1,16,128]{2,1,0:T(8,128)S(1)} %get-tuple-element.11, f32[1,16,128]{2,1,0:T(8,128)S(1)} %get-tuple-element.21, f32[1,16,128]{2,1,0:T(8,128)S(1)} %get-tuple-element.10, f32[1,18,1]{2,1,0:T(8,128)S(1)} %collective-permute-done.23, f32[1,1,128]{2,1,0:T(1,128)S(1)} %collective-permute-done.21, ...), kind=kLoop, calls=%fused_computation.128 | loop fusion | flops 79872 | bytes 107692 | tf_op jit(solution)/shard_map/mul | solution.py:108
  134.2 2.6 %collective-permute-start.27 = (bf16[1,18,1,128]{3,2,1,0:T(2,128)(2,1)S(1)}, bf16[1,18,1,128]{3,2,1,0:T(2,128)(2,1)S(1)}, u32[]{:S(2)}, u32[]{:S(2)}) collective-permute-start(bf16[1,18,1,128]{3,2,1,0:T(2,128)(2,1)S(1)} %get-tuple-element.43), channel_id=1, source_target_pairs={{1,0},{2,1},{3,2},{0,3},{5,4},{6,5},{7,6},{4,7},{9,8},{10,9},{11,1... | collective-permute-start | bytes 13832 | tf_op jit(solution)/shard_map/ppermute | solution.py:24
  146.9 2.2 collective-permute-start.28
  150.4 45.0 %all-reduce = (f32[128]{0:T(128)S(1)}, f32[128]{0:T(128)S(1)}) all-reduce(f32[128]{0:T(128)S(1)} %get-tuple-element.8, f32[128]{0:T(128)S(1)} %get-tuple-element.22), channel_id=1, replica_groups=mesh['dp'=2,'lat'=4,'lon'=4] {'dp','lat','lon'}, use_global_device_ids=true, to_apply=%region_7.0 | all-reduce | flops 256 | bytes 2048 | tf_op jit(solution)/shard_map/psum | solution.py:143
  196.0 2.4 %collective-permute-start.30 = (bf16[1,18,1,128]{3,2,1,0:T(2,128)(2,1)S(1)}, bf16[1,18,1,128]{3,2,1,0:T(2,128)(2,1)S(1)}, u32[]{:S(2)}, u32[]{:S(2)}) collective-permute-start(bf16[1,18,1,128]{3,2,1,0:T(2,128)(2,1)S(1)} %get-tuple-element.37), channel_id=1, source_target_pairs={{1,0},{2,1},{3,2},{0,3},{5,4},{6,5},{7,6},{4,7},{9,8},{10,9},{11,1... | collective-permute-start | bytes 13832 | tf_op jit(solution)/shard_map/ppermute | solution.py:24
  199.7 4.1 %collective-permute-done.31 = bf16[1,18,1,128]{3,2,1,0:T(2,128)(2,1)S(1)} collective-permute-done((bf16[1,18,1,128]{3,2,1,0:T(2,128)(2,1)S(1)}, bf16[1,18,1,128]{3,2,1,0:T(2,128)(2,1)S(1)}, u32[]{:S(2)}, u32[]{:S(2)}) %collective-permute-start.31) | collective-permute-done | bytes 4640 | tf_op jit(solution)/shard_map/ppermute | solution.py:22
  207.9 9.9 %psum.37 = f32[8,3,3,128]{3,0,2,1:T(8,128)S(1)} all-reduce(f32[8,3,3,128]{3,0,2,1:T(8,128)} %reduce-scatter.2.cloned.1.call-done), channel_id=1, replica_groups=mesh['dp'=2,'lat'=4,'lon'=4] {'dp'}, use_global_device_ids=true, to_apply=%region_5.0 | all-reduce | flops 9216 | bytes 73728 | tf_op jit(solution)/shard_map/psum | solution.py:142
  (129 shorter events, 55.3 us)
Async XLA Ops:
  7.2 200.7 %reduce-scatter.2.cloned.1.call-start = ((), (), s32[]{:S(2)}) async-start(), calls=%async_computation.1 | async-start | bytes 626688 | tf_op jit(solution)/shard_map/reduce_scatter | solution.py:136
  8.7 51.3 %collective-permute-start = (f32[2,1,128]{2,1,0:T(1,128)S(1)}, f32[2,1,128]{2,1,0:T(1,128)S(1)}, u32[]{:S(2)}, u32[]{:S(2)}) collective-permute-start(f32[2,1,128]{2,1,0:T(1,128)S(1)} %get-tuple-element.57), channel_id=1, source_target_pairs={{0,4},{4,8},{8,12},{1,5},{5,9},{9,13},{2,6},{6,10},{10,14},{3,7},{... | collective-permute-start | bytes 3080 | tf_op jit(solution)/shard_map/ppermute | solution.py:22
  11.1 49.0 %collective-permute-start.1 = (f32[2,1,128]{2,1,0:T(1,128)S(1)}, f32[2,1,128]{2,1,0:T(1,128)S(1)}, u32[]{:S(2)}, u32[]{:S(2)}) collective-permute-start(f32[2,1,128]{2,1,0:T(1,128)S(1)} %get-tuple-element.58), channel_id=1, source_target_pairs={{4,0},{8,4},{12,8},{5,1},{9,5},{13,9},{6,2},{10,6},{14,10},{7,3},{... | collective-permute-start | bytes 3080 | tf_op jit(solution)/shard_map/ppermute | solution.py:24
  53.6 5.6 %collective-permute-start.4 = (f32[1,1,128]{2,1,0:T(1,128)S(1)}, f32[1,1,128]{2,1,0:T(1,128)S(1)}, u32[]{:S(2)}, u32[]{:S(2)}) collective-permute-start(f32[1,1,128]{2,1,0:T(1,128)S(1)} %get-tuple-element.77), channel_id=1, source_target_pairs={{0,4},{4,8},{8,12},{1,5},{5,9},{9,13},{2,6},{6,10},{10,14},{3,7},{... | collective-permute-start | bytes 1544 | tf_op jit(solution)/shard_map/ppermute | solution.py:22
  54.9 5.0 %collective-permute-start.5 = (f32[1,1,128]{2,1,0:T(1,128)S(1)}, f32[1,1,128]{2,1,0:T(1,128)S(1)}, u32[]{:S(2)}, u32[]{:S(2)}) collective-permute-start(f32[1,1,128]{2,1,0:T(1,128)S(1)} %get-tuple-element.78), channel_id=1, source_target_pairs={{4,0},{8,4},{12,8},{5,1},{9,5},{13,9},{6,2},{10,6},{14,10},{7,3},{... | collective-permute-start | bytes 1544 | tf_op jit(solution)/shard_map/ppermute | solution.py:24
  60.0 7.5 %collective-permute-start.6 = (f32[1,18,1]{2,1,0:T(8,128)S(1)}, f32[1,18,1]{2,1,0:T(8,128)S(1)}, u32[]{:S(2)}, u32[]{:S(2)}) collective-permute-start(f32[1,18,1]{2,1,0:T(8,128)S(1)} %get-tuple-element.67), channel_id=1, source_target_pairs={{0,1},{1,2},{2,3},{3,0},{4,5},{5,6},{6,7},{7,4},{8,9},{9,10},{10,1... | collective-permute-start | bytes 224 | tf_op jit(solution)/shard_map/ppermute | solution.py:22
  60.8 5.8 %collective-permute-start.2 = (f32[2,18,1]{2,1,0:T(8,128)S(1)}, f32[2,18,1]{2,1,0:T(8,128)S(1)}, u32[]{:S(2)}, u32[]{:S(2)}) collective-permute-start(f32[2,18,1]{2,1,0:T(8,128)S(1)} %get-tuple-element.55), channel_id=1, source_target_pairs={{0,1},{1,2},{2,3},{3,0},{4,5},{5,6},{6,7},{7,4},{8,9},{9,10},{10,1... | collective-permute-start | bytes 440 | tf_op jit(solution)/shard_map/ppermute | solution.py:22
  61.0 5.7 %collective-permute-start.3 = (f32[2,18,1]{2,1,0:T(8,128)S(1)}, f32[2,18,1]{2,1,0:T(8,128)S(1)}, u32[]{:S(2)}, u32[]{:S(2)}) collective-permute-start(f32[2,18,1]{2,1,0:T(8,128)S(1)} %get-tuple-element.56), channel_id=1, source_target_pairs={{1,0},{2,1},{3,2},{0,3},{5,4},{6,5},{7,6},{4,7},{9,8},{10,9},{11,1... | collective-permute-start | bytes 440 | tf_op jit(solution)/shard_map/ppermute | solution.py:24
  72.3 6.0 %collective-permute-start.9 = (f32[1,1,128]{2,1,0:T(1,128)S(1)}, f32[1,1,128]{2,1,0:T(1,128)S(1)}, u32[]{:S(2)}, u32[]{:S(2)}) collective-permute-start(f32[1,1,128]{2,1,0:T(1,128)S(1)} %get-tuple-element.76), channel_id=1, source_target_pairs={{4,0},{8,4},{12,8},{5,1},{9,5},{13,9},{6,2},{10,6},{14,10},{7,3},{... | collective-permute-start | bytes 1544 | tf_op jit(solution)/shard_map/ppermute | solution.py:24
  78.4 5.5 %collective-permute-start.10 = (f32[1,18,1]{2,1,0:T(8,128)S(1)}, f32[1,18,1]{2,1,0:T(8,128)S(1)}, u32[]{:S(2)}, u32[]{:S(2)}) collective-permute-start(f32[1,18,1]{2,1,0:T(8,128)S(1)} %get-tuple-element.65), channel_id=1, source_target_pairs={{0,1},{1,2},{2,3},{3,0},{4,5},{5,6},{6,7},{7,4},{8,9},{9,10},{10,1... | collective-permute-start | bytes 224 | tf_op jit(solution)/shard_map/ppermute | solution.py:22
  78.4 5.5 %collective-permute-start.11 = (f32[1,18,1]{2,1,0:T(8,128)S(1)}, f32[1,18,1]{2,1,0:T(8,128)S(1)}, u32[]{:S(2)}, u32[]{:S(2)}) collective-permute-start(f32[1,18,1]{2,1,0:T(8,128)S(1)} %get-tuple-element.66), channel_id=1, source_target_pairs={{1,0},{2,1},{3,2},{0,3},{5,4},{6,5},{7,6},{4,7},{9,8},{10,9},{11,1... | collective-permute-start | bytes 224 | tf_op jit(solution)/shard_map/ppermute | solution.py:24
  85.2 4.6 %collective-permute-start.12 = (f32[1,1,128]{2,1,0:T(1,128)S(1)}, f32[1,1,128]{2,1,0:T(1,128)S(1)}, u32[]{:S(2)}, u32[]{:S(2)}) collective-permute-start(f32[1,1,128]{2,1,0:T(1,128)S(1)} %get-tuple-element.73), channel_id=1, source_target_pairs={{0,4},{4,8},{8,12},{1,5},{5,9},{9,13},{2,6},{6,10},{10,14},{3,7},{... | collective-permute-start | bytes 1544 | tf_op jit(solution)/shard_map/ppermute | solution.py:22
  92.2 5.5 %collective-permute-start.14 = (f32[1,18,1]{2,1,0:T(8,128)S(1)}, f32[1,18,1]{2,1,0:T(8,128)S(1)}, u32[]{:S(2)}, u32[]{:S(2)}) collective-permute-start(f32[1,18,1]{2,1,0:T(8,128)S(1)} %get-tuple-element.63), channel_id=1, source_target_pairs={{0,1},{1,2},{2,3},{3,0},{4,5},{5,6},{6,7},{7,4},{8,9},{9,10},{10,1... | collective-permute-start | bytes 224 | tf_op jit(solution)/shard_map/ppermute | solution.py:22
  99.0 4.7 %collective-permute-start.16 = (f32[1,1,128]{2,1,0:T(1,128)S(1)}, f32[1,1,128]{2,1,0:T(1,128)S(1)}, u32[]{:S(2)}, u32[]{:S(2)}) collective-permute-start(f32[1,1,128]{2,1,0:T(1,128)S(1)} %get-tuple-element.71), channel_id=1, source_target_pairs={{0,4},{4,8},{8,12},{1,5},{5,9},{9,13},{2,6},{6,10},{10,14},{3,7},{... | collective-permute-start | bytes 1544 | tf_op jit(solution)/shard_map/ppermute | solution.py:22
  106.0 5.5 %collective-permute-start.18 = (f32[1,18,1]{2,1,0:T(8,128)S(1)}, f32[1,18,1]{2,1,0:T(8,128)S(1)}, u32[]{:S(2)}, u32[]{:S(2)}) collective-permute-start(f32[1,18,1]{2,1,0:T(8,128)S(1)} %get-tuple-element.61), channel_id=1, source_target_pairs={{0,1},{1,2},{2,3},{3,0},{4,5},{5,6},{6,7},{7,4},{8,9},{9,10},{10,1... | collective-permute-start | bytes 224 | tf_op jit(solution)/shard_map/ppermute | solution.py:22
  112.8 9.5 %collective-permute-start.20 = (f32[1,1,128]{2,1,0:T(1,128)S(1)}, f32[1,1,128]{2,1,0:T(1,128)S(1)}, u32[]{:S(2)}, u32[]{:S(2)}) collective-permute-start(f32[1,1,128]{2,1,0:T(1,128)S(1)} %get-tuple-element.69), channel_id=1, source_target_pairs={{0,4},{4,8},{8,12},{1,5},{5,9},{9,13},{2,6},{6,10},{10,14},{3,7},{... | collective-permute-start | bytes 1544 | tf_op jit(solution)/shard_map/ppermute | solution.py:22
  116.2 6.1 %collective-permute-start.21 = (f32[1,1,128]{2,1,0:T(1,128)S(1)}, f32[1,1,128]{2,1,0:T(1,128)S(1)}, u32[]{:S(2)}, u32[]{:S(2)}) collective-permute-start(f32[1,1,128]{2,1,0:T(1,128)S(1)} %get-tuple-element.70), channel_id=1, source_target_pairs={{4,0},{8,4},{12,8},{5,1},{9,5},{13,9},{6,2},{10,6},{14,10},{7,3},{... | collective-permute-start | bytes 1544 | tf_op jit(solution)/shard_map/ppermute | solution.py:24
  117.5 14.9 %collective-permute-start.24 = (bf16[1,1,128,128]{3,2,1,0:T(8,128)(2,1)S(1)}, bf16[1,1,128,128]{3,2,1,0:T(8,128)(2,1)S(1)}, u32[]{:S(2)}, u32[]{:S(2)}) collective-permute-start(bf16[1,1,128,128]{3,2,1,0:T(8,128)(2,1)S(1)} %get-tuple-element.52), channel_id=1, source_target_pairs={{0,4},{4,8},{8,12},{1,5},{5,9},{9,13},{2,6},{6,10},{10,14},{3,7},{... | collective-permute-start | bytes 98312 | tf_op jit(solution)/shard_map/ppermute | solution.py:22
  121.0 11.5 %collective-permute-start.25 = (bf16[1,1,128,128]{3,2,1,0:T(8,128)(2,1)S(1)}, bf16[1,1,128,128]{3,2,1,0:T(8,128)(2,1)S(1)}, u32[]{:S(2)}, u32[]{:S(2)}) collective-permute-start(bf16[1,1,128,128]{3,2,1,0:T(8,128)(2,1)S(1)} %get-tuple-element.51), channel_id=1, source_target_pairs={{4,0},{8,4},{12,8},{5,1},{9,5},{13,9},{6,2},{10,6},{14,10},{7,3},{... | collective-permute-start | bytes 98312 | tf_op jit(solution)/shard_map/ppermute | solution.py:24
  122.4 5.5 %collective-permute-start.22 = (f32[1,18,1]{2,1,0:T(8,128)S(1)}, f32[1,18,1]{2,1,0:T(8,128)S(1)}, u32[]{:S(2)}, u32[]{:S(2)}) collective-permute-start(f32[1,18,1]{2,1,0:T(8,128)S(1)} %get-tuple-element.59), channel_id=1, source_target_pairs={{0,1},{1,2},{2,3},{3,0},{4,5},{5,6},{6,7},{7,4},{8,9},{9,10},{10,1... | collective-permute-start | bytes 224 | tf_op jit(solution)/shard_map/ppermute | solution.py:22
  132.9 5.6 %collective-permute-start.26 = (bf16[1,18,1,128]{3,2,1,0:T(2,128)(2,1)S(1)}, bf16[1,18,1,128]{3,2,1,0:T(2,128)(2,1)S(1)}, u32[]{:S(2)}, u32[]{:S(2)}) collective-permute-start(bf16[1,18,1,128]{3,2,1,0:T(2,128)(2,1)S(1)} %get-tuple-element.42), channel_id=1, source_target_pairs={{0,1},{1,2},{2,3},{3,0},{4,5},{5,6},{6,7},{7,4},{8,9},{9,10},{10,1... | collective-permute-start | bytes 13832 | tf_op jit(solution)/shard_map/ppermute | solution.py:22
  146.9 49.1 %collective-permute-start.28 = (bf16[1,1,128,128]{3,2,1,0:T(8,128)(2,1)S(1)}, bf16[1,1,128,128]{3,2,1,0:T(8,128)(2,1)S(1)}, u32[]{:S(2)}, u32[]{:S(2)}) collective-permute-start(bf16[1,1,128,128]{3,2,1,0:T(8,128)(2,1)S(1)} %get-tuple-element.46), channel_id=1, source_target_pairs={{0,4},{4,8},{8,12},{1,5},{5,9},{9,13},{2,6},{6,10},{10,14},{3,7},{... | collective-permute-start | bytes 98312 | tf_op jit(solution)/shard_map/ppermute | solution.py:22
  149.1 46.9 %collective-permute-start.29 = (bf16[1,1,128,128]{3,2,1,0:T(8,128)(2,1)S(1)}, bf16[1,1,128,128]{3,2,1,0:T(8,128)(2,1)S(1)}, u32[]{:S(2)}, u32[]{:S(2)}) collective-permute-start(bf16[1,1,128,128]{3,2,1,0:T(8,128)(2,1)S(1)} %get-tuple-element.47), channel_id=1, source_target_pairs={{4,0},{8,4},{12,8},{5,1},{9,5},{13,9},{6,2},{10,6},{14,10},{7,3},{... | collective-permute-start | bytes 98312 | tf_op jit(solution)/shard_map/ppermute | solution.py:24
  198.3 5.5 %collective-permute-start.31 = (bf16[1,18,1,128]{3,2,1,0:T(2,128)(2,1)S(1)}, bf16[1,18,1,128]{3,2,1,0:T(2,128)(2,1)S(1)}, u32[]{:S(2)}, u32[]{:S(2)}) collective-permute-start(bf16[1,18,1,128]{3,2,1,0:T(2,128)(2,1)S(1)} %get-tuple-element.38), channel_id=1, source_target_pairs={{0,1},{1,2},{2,3},{3,0},{4,5},{5,6},{6,7},{7,4},{8,9},{9,10},{10,1... | collective-permute-start | bytes 13832 | tf_op jit(solution)/shard_map/ppermute | solution.py:22
  (15 other events, 273.1 us)
Sparse Core Ops, SparseCore 0:
  147.0 57.9 reduce-scatter.1
where the time goes:
time: 227 us; the launch traced here: 225 us
  blocking collectives  91.5 us (40%)
  starting transfers between devices  60.1 us (26%)
  waiting for transfers between devices  23.7 us (10%)
  other arithmetic  18.9 us (8%)
  between operations  15.9 us (7%)
  matrix products  9.55 us (4%)
  local copies, waits for them, and re-layouts  5.66 us (2%)
    psum x1, blocking collectives, shards(): lax.psum((local_bias, local_proj), ('dp', 'lat', 'lon'))  45 us
    psum x1, blocking collectives, shards(): lax.psum((jnp.sum(mask_float), jnp.sum(mask_float * surface_cotangent, ax...  36.6 us
    ppermute x16, starting transfers between devices, extended(): lax.ppermute(head, axis, [((i + 1) % count, i) for i in range(ends)])  32.9 us
    ppermute x16, starting transfers between devices, extended(): lax.ppermute(tail, axis, [(i, (i + 1) % count) for i in range(ends)])  27.1 us
    ppermute x16, waiting for transfers between devices, extended(): lax.ppermute(tail, axis, [(i, (i + 1) % count) for i in range(ends)])  11.9 us
    ppermute x16, waiting for transfers between devices, extended(): lax.ppermute(head, axis, [((i + 1) % count, i) for i in range(ends)])  11.7 us
    psum x1, blocking collectives, shards(): own_weight = lax.psum(spatial, 'dp')  9.87 us
    add x4, other arithmetic, solve_steps(): direction = residual + step_beta[turn_index] * direction  5.32 us
  transfers between devices with their start and end apart: 33, of which 12 were waited for; matrix products, arithmetic and copies ran while one was open for 8% of the time, Pallas kernels for 0%

commit v1 on v0

v1 whole, which is shorter than its diff:
```python
import functools
import math

import jax
import jax.numpy as jnp
from jax import lax
from jax.experimental import pallas as pl
from jax.experimental.pallas import tpu as pltpu
from jax.sharding import PartitionSpec as P

MESH = pl.DeviceIdType.MESH
F32 = jnp.float32
BF16 = jnp.bfloat16
HALF = 8


def remote(src, dst, send, recv, device):
    return pltpu.make_async_remote_copy(
        src_ref=src, dst_ref=dst, send_sem=send, recv_sem=recv, device_id=device, device_id_type=MESH
    )


def kernel(dims, *refs):
    ndp, nlat, nlon, rows, cols, chan, iters, fast = dims
    (x_ref, w_ref, bias_ref, proj_ref, depth_ref, mask_ref, alpha_ref, beta_ref, ct_ref) = refs[:9]
    gh_ref, gw_ref, sum_ref = refs[9:12]
    (xs, gs, wb, fld, q_in, ebuf, el_in, ec_in, gbuf, gl_in, gc_in, mean_buf, small_buf, small_dp) = refs[12:26]
    (x_send, x_recv, g_send, g_recv, mean_send, mean_recv, small_send, small_recv, sdp_send, sdp_recv) = refs[26:36]
    if fast:
        (g1, r1, s1, r2, b3, r3, s4) = refs[36:43]
        (r1_send, r1_recv, r2_send, r2_recv, r3_send, r3_recv, r4_send, r4_recv) = refs[43:51]
    dp, la, lo = lax.axis_index("dp"), lax.axis_index("lat"), lax.axis_index("lon")
    group = nlat * nlon
    me = la * nlon + lo
    west, east = lax.rem(lo + nlon - 1, nlon), lax.rem(lo + 1, nlon)
    has_n, has_s = la > 0, la < nlat - 1

    def peer(step):
        spot = lax.rem(me + step, group)
        return spot, {"lat": spot // nlon, "lon": lax.rem(spot, nlon)}

    barrier = pltpu.get_barrier_semaphore()
    for step in range(1, group):
        pl.semaphore_signal(barrier, inc=1, device_id=peer(step)[1], device_id_type=MESH)
    for step in range(1, ndp):
        pl.semaphore_signal(barrier, inc=1, device_id={"dp": lax.rem(dp + step, ndp)}, device_id_type=MESH)

    mask = mask_ref[...].astype(F32)
    wet = mask * depth_ref[...]
    start = mask * ct_ref[0]
    fld[0] = wet
    fld[1] = start
    lane = lax.broadcasted_iota(jnp.int32, (rows, cols), 1)
    ebuf[1] = jnp.where(
        lane < 16,
        wet,
        jnp.where(lane < 64, pltpu.roll(start, 16, 1), jnp.where(lane < cols - 16, pltpu.roll(start, cols - 16, 1), wet)),
    )
    mean_buf[me] = jnp.concatenate(
        [jnp.sum(mask, axis=0, keepdims=True), jnp.sum(start, axis=0, keepdims=True)], axis=0
    )
    for row in range(rows):
        ebuf[0, row : row + 1, :] = x_ref[0, row, 0:16, :].astype(F32)[0:1]
        ebuf[2, row : row + 1, :] = x_ref[0, row, cols - 16 : cols, :].astype(F32)[15:16]

    pl.semaphore_wait(barrier, group - 1 + ndp - 1)

    def halo_copies(send, recv, row_pair, q_pair, line_pair, corner):
        north, south = {"lat": la - 1}, {"lat": la + 1}
        out = []
        out.append((has_n, has_s, remote(row_pair[0], row_pair[1], send.at[0], recv.at[0], north)))
        out.append((has_s, has_n, remote(row_pair[2], row_pair[3], send.at[1], recv.at[1], south)))
        for at in range(2):
            out.append((None, None, remote(line_pair[at][0], line_pair[at][1], send.at[2 + at], recv.at[2 + at], {"lon": (west, east)[at]})))
        for at in range(4):
            up = at < 2
            place = {"lat": la - 1 if up else la + 1, "lon": (west, east)[at % 2]}
            guards = (has_n, has_s) if up else (has_s, has_n)
            out.append(guards + (remote(corner[at][0], corner[at][1], send.at[4 + at], recv.at[4 + at], place),))
        if q_pair is not None:
            out.append((has_n, has_s, remote(q_pair[0], q_pair[1], send.at[8], recv.at[8], north)))
            out.append((has_s, has_n, remote(q_pair[2], q_pair[3], send.at[9], recv.at[9], south)))
        return out

    def guarded(guard, action):
        if guard is None:
            action()
        else:
            pl.when(guard)(action)

    def clear(guard, views):
        @pl.when(jnp.logical_not(guard))
        def _():
            for view in views:
                view[...] = jnp.zeros(view.shape, view.dtype)

    x_copies = halo_copies(
        x_send,
        x_recv,
        (x_ref.at[0, 0], xs.at[1, rows + 1], x_ref.at[0, rows - 1], xs.at[1, 0]),
        (fld.at[:, 0:HALF], q_in.at[0], fld.at[:, rows - HALF : rows], q_in.at[1]),
        ((ebuf.at[0:2], el_in.at[0]), (ebuf.at[1:3], el_in.at[1])),
        (
            (ebuf.at[0:2, 0:HALF], ec_in.at[0]),
            (ebuf.at[1:3, 0:HALF], ec_in.at[1]),
            (ebuf.at[0:2, rows - HALF : rows], ec_in.at[2]),
            (ebuf.at[1:3, rows - HALF : rows], ec_in.at[3]),
        ),
    )
    for at in (8, 9, 4, 5, 6, 7, 2, 3, 0, 1):
        guarded(x_copies[at][0], x_copies[at][2].start)
    mean_copies = []
    for step in range(1, group):
        spot, place = peer(step)
        mean_copies.append(remote(mean_buf.at[me], mean_buf.at[me], mean_send.at[step - 1], mean_recv.at[me], place))
        mean_copies[-1].start()
    clear(has_s, (xs.at[1, rows + 1], q_in.at[0], ec_in.at[0], ec_in.at[1]))
    clear(has_n, (xs.at[1, 0], q_in.at[1], ec_in.at[2], ec_in.at[3]))

    for tap in range(9):
        wb[tap * chan : (tap + 1) * chan, :] = w_ref[(8 - tap) * chan : (9 - tap) * chan, :].astype(F32).T.astype(BF16)
    for row in range(rows):
        own = x_ref[0, row]
        wide = own.astype(F32)
        xs[1, row + 1] = own
        xs[0, row + 1] = pltpu.roll(wide, 1, 0).astype(BF16)
        xs[2, row + 1] = pltpu.roll(wide, cols - 1, 0).astype(BF16)

    for at in range(10):
        guarded(x_copies[at][1], x_copies[at][2].wait_recv)

    tile_row = lax.broadcasted_iota(jnp.int32, (16, chan), 0)

    def fix(stack, row, left, right):
        head = stack[0, row, 0:16, :].astype(F32)
        stack[0, row, 0:16, :] = jnp.where(tile_row == 0, left, head).astype(BF16)
        tail = stack[2, row, cols - 16 : cols, :].astype(F32)
        stack[2, row, cols - 16 : cols, :] = jnp.where(tile_row == 15, right, tail).astype(BF16)

    def fix_ends(stack, top, bottom):
        for row, (left, right) in ((0, top), (rows + 1, bottom)):
            wide = stack[1, row].astype(F32)
            stack[0, row] = pltpu.roll(wide, 1, 0).astype(BF16)
            stack[2, row] = pltpu.roll(wide, cols - 1, 0).astype(BF16)
            fix(stack, row, left, right)

    last = HALF - 1
    fix_ends(
        xs,
        (ec_in[3, 1, last : last + 1, :], ec_in[2, 0, last : last + 1, :]),
        (ec_in[1, 1, 0:1, :], ec_in[0, 0, 0:1, :]),
    )
    for row in range(rows):
        fix(xs, row + 1, el_in[1, 1, row : row + 1, :], el_in[0, 0, row : row + 1, :])

    tall = rows + 2 * HALF
    side_lane = lax.broadcasted_iota(jnp.int32, (tall, cols), 1)
    from_west = jnp.concatenate([ec_in[3, 0], el_in[1, 0], ec_in[1, 0]], axis=0)
    from_east = jnp.concatenate([ec_in[2, 1], el_in[0, 1], ec_in[0, 1]], axis=0)
    near = jnp.logical_or(side_lane < iters - 1, side_lane >= cols - (iters - 1))
    wet_side = jnp.where(near, jnp.where(side_lane < 64, from_east, from_west), 0.0)
    start_side = jnp.where(
        near, jnp.where(side_lane < 64, pltpu.roll(from_east, cols - 16, 1), pltpu.roll(from_west, 16, 1)), 0.0
    )
    wet_all = jnp.concatenate([jnp.concatenate([q_in[1, 0], fld[0], q_in[0, 0]], axis=0), wet_side], axis=1)
    start_all = jnp.concatenate([jnp.concatenate([q_in[1, 1], fld[1], q_in[0, 1]], axis=0), start_side], axis=1)
    turns = ((1, 0), (tall - 1, 0), (1, 1), (2 * cols - 1, 1))
    mask_all = jnp.where(wet_all > 0.0, 1.0, 0.0)
    weights = [
        mask_all * pltpu.roll(mask_all, shift, axis) * (0.5 * (wet_all + pltpu.roll(wet_all, shift, axis)))
        for shift, axis in turns
    ]
    diagonal = 0.5 * mask_all + ((weights[0] + weights[1]) + (weights[2] + weights[3]))
    found = []
    for begin in (start_all, mask_all):
        residual = direction = begin
        answer = jnp.zeros_like(begin)
        for turn in range(iters):
            answer = answer + alpha_ref[turn] * direction
            if turn + 1 < iters:
                applied = diagonal * direction
                for weight, (shift, axis) in zip(weights, turns):
                    applied = applied - weight * pltpu.roll(direction, shift, axis)
                residual = residual - alpha_ref[turn] * applied
                direction = residual + beta_ref[turn] * direction
        found.append(answer[HALF : HALF + rows, 0:cols])

    def forward(first, count):
        lhs = jnp.concatenate(
            [
                xs[c, first + a : first + a + count].reshape(count * cols, chan)
                for a in range(3)
                for c in range(3)
            ],
            axis=1,
        )
        return jnp.dot(lhs, w_ref[...], preferred_element_type=F32) + bias_ref[...]

    for step in range(1, group):
        spot, place = peer(step)
        remote(mean_buf.at[spot], mean_buf.at[spot], mean_send.at[step - 1], mean_recv.at[spot], place).wait_recv()
    total = jnp.sum(mean_buf[...], axis=0)
    mean = jnp.sum(total[1:2, :], axis=1, keepdims=True) / jnp.sum(total[0:1, :], axis=1, keepdims=True)
    forcing = mask * (found[0] - mean * found[1])
    columns = forcing.T

    block = 4
    bias_sum = jnp.zeros((HALF, chan), F32)
    proj_sum = jnp.zeros((HALF, chan), F32)
    for first in range(0, rows, block):
        preact = forward(first, block)
        for at in range(block):
            row = first + at
            pre = preact[at * cols : (at + 1) * cols]
            sigma = jax.nn.sigmoid(pre)
            force = jnp.broadcast_to(columns[:, row : row + 1], (cols, chan))
            active = pre * sigma
            cotangent = (force * proj_ref[...] * (sigma * (1.0 + pre * (1.0 - sigma)))).astype(BF16)
            gs[1, row + 1] = cotangent
            wide = cotangent.astype(F32)
            gbuf[0, row : row + 1, :] = wide[0:1]
            gbuf[1, row : row + 1, :] = wide[cols - 1 : cols]
            bias_sum = bias_sum + jnp.sum(wide.reshape(cols // HALF, HALF, chan), axis=0)
            proj_sum = proj_sum + jnp.sum((active * force).reshape(cols // HALF, HALF, chan), axis=0)
    small_buf[me] = jnp.concatenate(
        [jnp.sum(bias_sum, axis=0, keepdims=True), jnp.sum(proj_sum, axis=0, keepdims=True)], axis=0
    )

    g_copies = halo_copies(
        g_send,
        g_recv,
        (gs.at[1, 1], gs.at[1, rows + 1], gs.at[1, rows], gs.at[1, 0]),
        None,
        ((gbuf.at[0], gl_in.at[0]), (gbuf.at[1], gl_in.at[1])),
        (
            (gbuf.at[0, 0:HALF], gc_in.at[0]),
            (gbuf.at[1, 0:HALF], gc_in.at[1]),
            (gbuf.at[0, rows - HALF : rows], gc_in.at[2]),
            (gbuf.at[1, rows - HALF : rows], gc_in.at[3]),
        ),
    )
    for at in (4, 5, 6, 7, 2, 3, 0, 1):
        guarded(g_copies[at][0], g_copies[at][2].start)
    small_copies = []
    for step in range(1, group):
        spot, place = peer(step)
        small_copies.append(remote(small_buf.at[me], small_buf.at[me], small_send.at[step - 1], small_recv.at[me], place))
        small_copies[-1].start()
    clear(has_s, (gs.at[1, rows + 1], gc_in.at[0], gc_in.at[1]))
    clear(has_n, (gs.at[1, 0], gc_in.at[2], gc_in.at[3]))

    right = gs[1, 1 : rows + 1].reshape(rows * cols, chan)
    pairs = nlat // 2
    own_lat = chan // nlat
    parity, half_at = lax.rem(la, 2), la // 2
    sends = []
    for a in range(3):
        for c in range(3):
            left = xs[c, a : a + rows].reshape(rows * cols, chan)
            part = lax.dot_general(left, right, (((0,), (0,)), ((), ())), preferred_element_type=F32)
            if fast:
                for lat_at in range(nlat):
                    g1[lat_at, 3 * a + c] = part[lat_at * own_lat : (lat_at + 1) * own_lat].astype(BF16)
            else:
                gw_ref[3 * a + c] = part
        if fast:
            for pair in range(pairs):
                sends.append(
                    remote(
                        g1.at[2 * pair + 1 - parity, 3 * a : 3 * a + 3],
                        r1.at[pair, 3 * a : 3 * a + 3],
                        r1_send.at[3 * pair + a],
                        r1_recv.at[3 * pair + a],
                        {"lat": la + 1 - 2 * parity},
                    )
                )
                sends[-1].start()
    first_stage = list(sends)

    for row in range(rows):
        wide = gs[1, row + 1].astype(F32)
        gs[0, row + 1] = pltpu.roll(wide, 1, 0).astype(BF16)
        gs[2, row + 1] = pltpu.roll(wide, cols - 1, 0).astype(BF16)

    second_stage = []
    if fast:
        for copy in first_stage:
            copy.wait_recv()
        for step in range(1, pairs):
            other = lax.rem(half_at + step, pairs)
            s1[step] = (g1[2 * other + parity].astype(F32) + r1[other].astype(F32)).astype(BF16)
            second_stage.append(
                remote(s1.at[step], r2.at[step], r2_send.at[step], r2_recv.at[step], {"lat": 2 * other + parity})
            )
            second_stage[-1].start()

    for at in range(8):
        guarded(g_copies[at][1], g_copies[at][2].wait_recv)
    fix_ends(
        gs,
        (gc_in[3, last : last + 1, :], gc_in[2, last : last + 1, :]),
        (gc_in[1, 0:1, :], gc_in[0, 0:1, :]),
    )
    for row in range(rows):
        fix(gs, row + 1, gl_in[1, row : row + 1, :], gl_in[0, row : row + 1, :])

    def backward(first, count):
        lhs = jnp.concatenate(
            [
                gs[c, first + a : first + a + count].reshape(count * cols, chan)
                for a in range(3)
                for c in range(3)
            ],
            axis=1,
        )
        result = jnp.dot(lhs, wb[...], preferred_element_type=F32).astype(BF16)
        gh_ref[0, first : first + count] = result.reshape(count, cols, chan)

    for step in range(1, group):
        spot, place = peer(step)
        remote(small_buf.at[spot], small_buf.at[spot], small_send.at[step - 1], small_recv.at[spot], place).wait_recv()
    small_dp[dp] = jnp.sum(small_buf[...], axis=0)
    small_dp_copies = []
    for step in range(1, ndp):
        place = {"dp": lax.rem(dp + step, ndp)}
        small_dp_copies.append(remote(small_dp.at[dp], small_dp.at[dp], sdp_send.at[step - 1], sdp_recv.at[dp], place))
        small_dp_copies[-1].start()

    quarter = rows // 4
    backward(0, quarter)
    third_stage, fourth_stage = [], []
    if fast:
        share = own_lat // nlon
        lat_sum = g1[2 * half_at + parity].astype(F32) + r1[half_at].astype(F32)
        for copy in second_stage:
            copy.wait_recv()
        for step in range(1, pairs):
            lat_sum = lat_sum + r2[step].astype(F32)
        for lon_at in range(nlon):
            b3[lon_at] = jnp.concatenate(
                [lat_sum[tap, lon_at * share : (lon_at + 1) * share] for tap in range(9)], axis=0
            ).astype(BF16)
        for step in range(1, nlon):
            other = lax.rem(lo + step, nlon)
            third_stage.append(remote(b3.at[other], r3.at[step], r3_send.at[step], r3_recv.at[step], {"lon": other}))
            third_stage[-1].start()
    backward(quarter, quarter)
    backward(2 * quarter, quarter)
    if fast:
        for copy in third_stage:
            copy.wait_recv()
        lon_sum = b3[lo].astype(F32)
        for step in range(1, nlon):
            lon_sum = lon_sum + r3[step].astype(F32)
        s4[dp] = lon_sum.astype(BF16)
        for step in range(1, ndp):
            place = {"dp": lax.rem(dp + step, ndp)}
            fourth_stage.append(remote(s4.at[dp], s4.at[dp], r4_send.at[step - 1], r4_recv.at[dp], place))
            fourth_stage[-1].start()
    backward(3 * quarter, quarter)

    cells = ndp * nlat * nlon * rows * cols
    scale = 1.0 / math.sqrt(cells)
    for step in range(1, ndp):
        other = lax.rem(dp + step, ndp)
        remote(small_dp.at[other], small_dp.at[other], sdp_send.at[step - 1], sdp_recv.at[other], {"dp": other}).wait_recv()
        if fast:
            remote(s4.at[other], s4.at[other], r4_send.at[step - 1], r4_recv.at[other], {"dp": other}).wait_recv()
    if fast:
        gw_ref[...] = jnp.sum(s4[...].astype(F32), axis=0) * scale
    sum_ref[...] = jnp.sum(small_dp[...], axis=0) * scale

    for guard, _, copy in x_copies + g_copies:
        guarded(guard, copy.wait_send)
    for copy in mean_copies + small_copies + small_dp_copies + first_stage + second_stage + third_stage + fourth_stage:
        copy.wait_send()


def shards(hidden_in, conv_weight, conv_bias, proj_weight, ocean_depth, sea_mask, step_alpha, step_beta, surface_cotangent):
    _, rows, cols, chan = hidden_in.shape
    ndp, nlat, nlon = (lax.axis_size(axis) for axis in ("dp", "lat", "lon"))
    group = nlat * nlon
    own_lat = chan // nlat
    share = own_lat // nlon
    fast = nlat % 2 == 0 and own_lat % 16 == 0 and share % 8 == 0
    iters = step_alpha.shape[0]
    dims = (ndp, nlat, nlon, rows, cols, chan, iters, fast)
    dma = lambda count: pltpu.SemaphoreType.DMA((max(count, 1),))
    scratch = [
        pltpu.VMEM((3, rows + 2, cols, chan), BF16),
        pltpu.VMEM((3, rows + 2, cols, chan), BF16),
        pltpu.VMEM((9 * chan, chan), BF16),
        pltpu.VMEM((2, rows, cols), F32),
        pltpu.VMEM((2, 2, HALF, cols), F32),
        pltpu.VMEM((3, rows, chan), F32),
        pltpu.VMEM((2, 2, rows, chan), F32),
        pltpu.VMEM((4, 2, HALF, chan), F32),
        pltpu.VMEM((2, rows, chan), F32),
        pltpu.VMEM((2, rows, chan), F32),
        pltpu.VMEM((4, HALF, chan), F32),
        pltpu.VMEM((group, 2, cols), F32),
        pltpu.VMEM((group, 2, chan), F32),
        pltpu.VMEM((ndp, 2, chan), F32),
        dma(10), dma(10), dma(8), dma(8),
        dma(group), dma(group), dma(group), dma(group), dma(ndp), dma(ndp),
    ]
    if fast:
        pairs = nlat // 2
        scratch += [
            pltpu.VMEM((nlat, 9, own_lat, chan), BF16),
            pltpu.VMEM((pairs, 9, own_lat, chan), BF16),
            pltpu.VMEM((pairs, 9, own_lat, chan), BF16),
            pltpu.VMEM((pairs, 9, own_lat, chan), BF16),
            pltpu.VMEM((nlon, 9 * share, chan), BF16),
            pltpu.VMEM((nlon, 9 * share, chan), BF16),
            pltpu.VMEM((ndp, 9 * share, chan), BF16),
            dma(3 * pairs), dma(3 * pairs), dma(pairs), dma(pairs), dma(nlon), dma(nlon), dma(ndp), dma(ndp),
        ]
    vmem, smem = pl.BlockSpec(memory_space=pltpu.VMEM), pl.BlockSpec(memory_space=pltpu.SMEM)
    gw_shape = (9 * share, chan) if fast else (9, chan, chan)
    grad_hidden, weight_part, sums = pl.pallas_call(
        functools.partial(kernel, dims),
        out_shape=(
            jax.ShapeDtypeStruct(hidden_in.shape, BF16),
            jax.ShapeDtypeStruct(gw_shape, F32),
            jax.ShapeDtypeStruct((2, chan), F32),
        ),
        in_specs=[vmem] * 6 + [smem] * 2 + [vmem],
        out_specs=(vmem, vmem, vmem),
        scratch_shapes=scratch,
        compiler_params=pltpu.CompilerParams(collective_id=0, has_side_effects=True, vmem_limit_bytes=48 * 1024 * 1024),
    )(
        hidden_in,
        conv_weight.reshape(9 * chan, chan),
        conv_bias.reshape(1, chan),
        proj_weight.reshape(1, chan),
        ocean_depth,
        sea_mask,
        step_alpha,
        step_beta,
        surface_cotangent,
    )
    if fast:
        grad_weight = weight_part.reshape(3, 3, share, chan).transpose(2, 0, 1, 3)
    else:
        blocks = weight_part.reshape(3, 3, chan, chan).transpose(2, 0, 1, 3)
        spatial = lax.psum_scatter(blocks, ("lat", "lon"), scatter_dimension=0, tiled=True)
        grad_weight = lax.psum(spatial, "dp") * (1.0 / math.sqrt(ndp * group * rows * cols))
    return grad_hidden, grad_weight, sums[0], sums[1]


def solution(mesh):
    in_specs = (
        P("dp", "lat", "lon", None),
        P(),
        P(),
        P(),
        P("lat", "lon"),
        P("lat", "lon"),
        P(),
        P(),
        P("dp", "lat", "lon"),
    )
    out_specs = (P("dp", "lat", "lon", None), P(("lat", "lon"), None, None, None), P(), P())
    return jax.shard_map(shards, mesh=mesh, in_specs=in_specs, out_specs=out_specs, check_vma=False)
```

time: 227 us -> 35.6 us (0.16)
  blocking collectives: 91.5 us -> 0 us
  starting transfers between devices: 60.1 us -> 0 us
  Pallas kernels: 0 us -> 27.9 us
  waiting for transfers between devices: 23.7 us -> 0 us
  other arithmetic: 18.9 us -> 0 us
  between operations: 15.9 us -> 0.68 us
  matrix products: 9.55 us -> 0 us
    psum x3 -> x0, blocking collectives: 91.5 us -> none  [the longest x1 45 us: shards(): lax.psum((local_bias, local_proj), ('dp', 'lat', 'lon'))]
    ppermute x32 -> x0, starting transfers between devices: 60 us -> none  [the longest x16 32.9 us: extended(): lax.ppermute(head, axis, [((i + 1) % count, i) for i in range(ends)])]
    pallas_call x0 -> x1, Pallas kernels: none -> 27.9 us  [shards(): pl.pallas_call(functools.partial(kernel, dims), out_shape=(jax.ShapeDtype...]
    ppermute x32 -> x0, waiting for transfers between devices: 23.7 us -> none  [the longest x16 11.9 us: extended(): lax.ppermute(tail, axis, [(i, (i + 1) % count) for i in range(ends)])]
    dot_general x27 -> x0, matrix products: 9.55 us -> none  [the longest x9 3.45 us: shards(): lax.dot_general(window, conv_weight[row_off, col_off], (((1,), (1,)), (()...]
    mul x4 -> x0, other arithmetic: 6.33 us -> none  [the longest x1 4.47 us: shards(): grad_pre = (force_col * proj_weight * slope_act).astype(jnp.bfloat16)]
    add x4 -> x0, other arithmetic: 5.32 us -> none  [solve_steps(): direction = residual + step_beta[turn_index] * direction]
    unnamed x13 -> x20, local copies, waits for them, and re-layouts: 1.55 us -> 6.17 us
  transfers between devices with their start and end apart: 33 -> 0, of which waited for: 12 -> 0; matrix products, arithmetic and copies ran while one was open for 8% -> 0% of each run, Pallas kernels for 0% -> 0%
where the time goes in v1:
time: 35.6 us; the launch traced here: 35.3 us
  Pallas kernels  27.9 us (78%)
  local copies, waits for them, and re-layouts  6.69 us (19%)
  between operations  0.68 us (2%)
    pallas_call x1, Pallas kernels, shards(): pl.pallas_call(functools.partial(kernel, dims), out_shape=(jax.ShapeDtype...  27.9 us
    unnamed x20, local copies, waits for them, and re-layouts  6.17 us

profile of v1, /device:TPU:0, one launch (start us, length us, event | category | flops | bytes accessed | tf_op | source)
XLA Modules:
  0.0 35.3 jit_solution(6679925180499281707)
XLA Ops:
  0.6 0.0 copy-start.8
  0.6 0.0 copy-start.5
  0.7 0.0 copy-start.6
  0.7 0.0 copy-start.7
  0.7 0.6 %copy-done.8 = f32[6]{0:T(128)S(1)} copy-done((f32[6]{0:T(128)S(1)}, f32[6]{0:T(128)}, u32[]{:S(2)}) %copy-start.8) | copy-done | bytes 48
  1.3 0.0 copy-done.5
  1.3 0.0 copy-done.6
  1.3 0.0 copy-done.7
  1.3 0.0 copy-start
  1.3 1.0 %copy-done = bf16[1,16,128,128]{3,2,1,0:T(8,128)(2,1)S(1)} copy-done((bf16[1,16,128,128]{3,2,1,0:T(8,128)(2,1)S(1)}, bf16[1,16,128,128]{3,2,1,0:T(8,128)(2,1)}, u32[]{:S(2)}) %copy-start) | copy-done | bytes 524312
  2.4 0.0 copy-start.1
  2.4 1.0 %copy-done.1 = bf16[3,3,128,128]{3,2,1,0:T(8,128)(2,1)S(1)} copy-done((bf16[3,3,128,128]{3,2,1,0:T(8,128)(2,1)S(1)}, bf16[3,3,128,128]{3,2,1,0:T(8,128)(2,1)}, u32[]{:S(2)}) %copy-start.1) | copy-done | bytes 294936
  3.3 0.0 copy-start.2
  3.3 0.7 %copy-done.2 = f32[16,128]{1,0:T(8,128)S(1)} copy-done((f32[16,128]{1,0:T(8,128)S(1)}, f32[16,128]{1,0:T(8,128)}, u32[]{:S(2)}) %copy-start.2) | copy-done | bytes 8216
  4.0 0.0 copy-start.3
  4.0 0.7 %copy-done.3 = s32[16,128]{1,0:T(8,128)S(1)} copy-done((s32[16,128]{1,0:T(8,128)S(1)}, s32[16,128]{1,0:T(8,128)}, u32[]{:S(2)}) %copy-start.3) | copy-done | bytes 8216
  4.7 0.0 copy-start.4
  4.7 0.7 %copy-done.4 = f32[1,16,128]{2,1,0:T(8,128)S(1)} copy-done((f32[1,16,128]{2,1,0:T(8,128)S(1)}, f32[1,16,128]{2,1,0:T(8,128)}, u32[]{:S(2)}) %copy-start.4) | copy-done | bytes 8216
  5.4 27.9 %shard_map.120 = (bf16[1,16,128,128]{3,2,1,0:T(8,128)(2,1)S(1)}, f32[72,128]{1,0:T(8,128)S(1)}, f32[2,128]{1,0:T(2,128)S(1)}) custom-call(bf16[1,16,128,128]{3,2,1,0:T(8,128)(2,1)S(1)} %copy-done, bf16[1152,128]{1,0:T(8,128)(2,1)S(1)} %bitcast.10, f32[1,128]{1,0:T(1,128)S(1)} %bitcast.12, f32[1,128]{1,0:T(1,128)S(1)} %bitcast.13, f32[16,128]{1,0:T(8,128)S(1)} %copy-done.2, ...), custom_call_target="tpu_custom_call" | custom-call | tf_op jit(solution)/shard_map/pallas_call | solution.py:421
  33.3 0.5 %slice_bitcast_fusion = (f32[128]{0:T(128)}, f32[128]{0:T(128)}) fusion(f32[2,128]{1,0:T(2,128)S(1)} %get-tuple-element.9), kind=kLoop, calls=%fused_computation | loop fusion | bytes 2048 | tf_op jit(solution)/shard_map/squeeze | solution.py:449
  33.9 0.8 %copy.15 = bf16[1,16,128,128]{3,2,1,0:T(8,128)(2,1)} copy(bf16[1,16,128,128]{3,2,1,0:T(8,128)(2,1)S(1)} %get-tuple-element.16) | data formatting | bytes 1048576
  34.7 0.6 %copy.16 = f32[8,3,3,128]{3,0,2,1:T(8,128)} copy(f32[8,3,3,128]{3,0,2,1:T(8,128)S(1)} %bitcast.11) | data formatting | bytes 73728
Async XLA Ops:
  0.6 0.7 %copy-start.8 = (f32[6]{0:T(128)S(1)}, f32[6]{0:T(128)}, u32[]{:S(2)}) copy-start(f32[6]{0:T(128)} %refs_7_.1) | copy-start | bytes 76
  0.6 0.7 %copy-start.5 = (f32[128]{0:T(128)S(1)}, f32[128]{0:T(128)}, u32[]{:S(2)}) copy-start(f32[128]{0:T(128)} %param.11) | copy-start | bytes 1540
  0.7 0.7 %copy-start.6 = (f32[128]{0:T(128)S(1)}, f32[128]{0:T(128)}, u32[]{:S(2)}) copy-start(f32[128]{0:T(128)} %param.12) | copy-start | bytes 1540
  0.7 0.7 %copy-start.7 = (f32[6]{0:T(128)S(1)}, f32[6]{0:T(128)}, u32[]{:S(2)}) copy-start(f32[6]{0:T(128)} %refs_6_.1) | copy-start | bytes 76
  1.3 1.0 %copy-start = (bf16[1,16,128,128]{3,2,1,0:T(8,128)(2,1)S(1)}, bf16[1,16,128,128]{3,2,1,0:T(8,128)(2,1)}, u32[]{:S(2)}) copy-start(bf16[1,16,128,128]{3,2,1,0:T(8,128)(2,1)} %refs_0_.1) | copy-start | bytes 1572868
  2.4 1.0 %copy-start.1 = (bf16[3,3,128,128]{3,2,1,0:T(8,128)(2,1)S(1)}, bf16[3,3,128,128]{3,2,1,0:T(8,128)(2,1)}, u32[]{:S(2)}) copy-start(bf16[3,3,128,128]{3,2,1,0:T(8,128)(2,1)} %param.10) | copy-start | bytes 884740
  3.3 0.7 %copy-start.2 = (f32[16,128]{1,0:T(8,128)S(1)}, f32[16,128]{1,0:T(8,128)}, u32[]{:S(2)}) copy-start(f32[16,128]{1,0:T(8,128)} %refs_4_.1) | copy-start | bytes 24580
  4.0 0.7 %copy-start.3 = (s32[16,128]{1,0:T(8,128)S(1)}, s32[16,128]{1,0:T(8,128)}, u32[]{:S(2)}) copy-start(s32[16,128]{1,0:T(8,128)} %refs_5_.1) | copy-start | bytes 24580
  4.7 0.7 %copy-start.4 = (f32[1,16,128]{2,1,0:T(8,128)S(1)}, f32[1,16,128]{2,1,0:T(8,128)}, u32[]{:S(2)}) copy-start(f32[1,16,128]{2,1,0:T(8,128)} %refs_8_.1) | copy-start | bytes 24580

commit v2 on v1

--- a/solution.py
+++ b/solution.py
@@ -22,13 +22,14 @@
 
 def kernel(dims, *refs):
     ndp, nlat, nlon, rows, cols, chan, iters, fast = dims
-    (x_ref, w_ref, bias_ref, proj_ref, depth_ref, mask_ref, alpha_ref, beta_ref, ct_ref) = refs[:9]
+    (x_hbm, w_hbm, bias_ref, proj_ref, depth_hbm, mask_hbm, alpha_ref, beta_ref, ct_hbm) = refs[:9]
     gh_ref, gw_ref, sum_ref = refs[9:12]
     (xs, gs, wb, fld, q_in, ebuf, el_in, ec_in, gbuf, gl_in, gc_in, mean_buf, small_buf, small_dp) = refs[12:26]
     (x_send, x_recv, g_send, g_recv, mean_send, mean_recv, small_send, small_recv, sdp_send, sdp_recv) = refs[26:36]
+    (x_ref, w_ref, depth_ref, mask_ref, ct_ref, load_sem, pre_buf) = refs[36:43]
     if fast:
-        (g1, r1, s1, r2, b3, r3, s4) = refs[36:43]
-        (r1_send, r1_recv, r2_send, r2_recv, r3_send, r3_recv, r4_send, r4_recv) = refs[43:51]
+        (g1, r1, s1, r2, b3, r3, s4) = refs[43:50]
+        (r1_send, r1_recv, r2_send, r2_recv, r3_send, r3_recv, r4_send, r4_recv) = refs[50:58]
     dp, la, lo = lax.axis_index("dp"), lax.axis_index("lat"), lax.axis_index("lon")
     group = nlat * nlon
     me = la * nlon + lo
@@ -39,12 +40,19 @@
         spot = lax.rem(me + step, group)
         return spot, {"lat": spot // nlon, "lon": lax.rem(spot, nlon)}
 
+    held = ((mask_hbm, mask_ref), (depth_hbm, depth_ref), (ct_hbm, ct_ref), (x_hbm, x_ref), (w_hbm, w_ref))
+    loads = [pltpu.make_async_copy(hbm, ref, load_sem.at[at]) for at, (hbm, ref) in enumerate(held)]
+    for load in loads:
+        load.start()
+
     barrier = pltpu.get_barrier_semaphore()
     for step in range(1, group):
         pl.semaphore_signal(barrier, inc=1, device_id=peer(step)[1], device_id_type=MESH)
     for step in range(1, ndp):
         pl.semaphore_signal(barrier, inc=1, device_id={"dp": lax.rem(dp + step, ndp)}, device_id_type=MESH)
 
+    for load in loads[:3]:
+        load.wait()
     mask = mask_ref[...].astype(F32)
     wet = mask * depth_ref[...]
     start = mask * ct_ref[0]
@@ -59,6 +67,7 @@
     mean_buf[me] = jnp.concatenate(
         [jnp.sum(mask, axis=0, keepdims=True), jnp.sum(start, axis=0, keepdims=True)], axis=0
     )
+    loads[3].wait()
     for row in range(rows):
         ebuf[0, row : row + 1, :] = x_ref[0, row, 0:16, :].astype(F32)[0:1]
         ebuf[2, row : row + 1, :] = x_ref[0, row, cols - 16 : cols, :].astype(F32)[15:16]
@@ -107,16 +116,17 @@
             (ebuf.at[1:3, rows - HALF : rows], ec_in.at[3]),
         ),
     )
-    for at in (8, 9, 4, 5, 6, 7, 2, 3, 0, 1):
-        guarded(x_copies[at][0], x_copies[at][2].start)
     mean_copies = []
     for step in range(1, group):
         spot, place = peer(step)
         mean_copies.append(remote(mean_buf.at[me], mean_buf.at[me], mean_send.at[step - 1], mean_recv.at[me], place))
         mean_copies[-1].start()
+    for at in (8, 9, 4, 5, 6, 7, 2, 3, 0, 1):
+        guarded(x_copies[at][0], x_copies[at][2].start)
     clear(has_s, (xs.at[1, rows + 1], q_in.at[0], ec_in.at[0], ec_in.at[1]))
     clear(has_n, (xs.at[1, 0], q_in.at[1], ec_in.at[2], ec_in.at[3]))
 
+    loads[4].wait()
     for tap in range(9):
         wb[tap * chan : (tap + 1) * chan, :] = w_ref[(8 - tap) * chan : (9 - tap) * chan, :].astype(F32).T.astype(BF16)
     for row in range(rows):
@@ -152,6 +162,21 @@
     )
     for row in range(rows):
         fix(xs, row + 1, el_in[1, 1, row : row + 1, :], el_in[0, 0, row : row + 1, :])
+
+    def forward(first, count):
+        lhs = jnp.concatenate(
+            [
+                xs[c, first + a : first + a + count].reshape(count * cols, chan)
+                for a in range(3)
+                for c in range(3)
+            ],
+            axis=1,
+        )
+        return jnp.dot(lhs, w_ref[...], preferred_element_type=F32) + bias_ref[...]
+
+    block = 4
+    for first in range(0, rows, block):
+        pre_buf[first * cols : (first + block) * cols, :] = forward(first, block)
 
     tall = rows + 2 * HALF
     side_lane = lax.broadcasted_iota(jnp.int32, (tall, cols), 1)
@@ -185,17 +210,6 @@
                 direction = residual + beta_ref[turn] * direction
         found.append(answer[HALF : HALF + rows, 0:cols])
 
-    def forward(first, count):
-        lhs = jnp.concatenate(
-            [
-                xs[c, first + a : first + a + count].reshape(count * cols, chan)
-                for a in range(3)
-                for c in range(3)
-            ],
-            axis=1,
-        )
-        return jnp.dot(lhs, w_ref[...], preferred_element_type=F32) + bias_ref[...]
-
     for step in range(1, group):
         spot, place = peer(step)
         remote(mean_buf.at[spot], mean_buf.at[spot], mean_send.at[step - 1], mean_recv.at[spot], place).wait_recv()
@@ -204,14 +218,12 @@
     forcing = mask * (found[0] - mean * found[1])
     columns = forcing.T
 
-    block = 4
     bias_sum = jnp.zeros((HALF, chan), F32)
     proj_sum = jnp.zeros((HALF, chan), F32)
     for first in range(0, rows, block):
-        preact = forward(first, block)
         for at in range(block):
             row = first + at
-            pre = preact[at * cols : (at + 1) * cols]
+            pre = pre_buf[row * cols : (row + 1) * cols, :]
             sigma = jax.nn.sigmoid(pre)
             force = jnp.broadcast_to(columns[:, row : row + 1], (cols, chan))
             active = pre * sigma
@@ -276,23 +288,71 @@
                 )
                 sends[-1].start()
     first_stage = list(sends)
+    second_stage, third_stage, fourth_stage = [], [], []
+    share = own_lat // nlon
+
+    def run_second(a):
+        taps = pl.ds(3 * a, 3)
+        for pair in range(pairs):
+            first_stage[a * pairs + pair].wait_recv()
+        for step in range(1, pairs):
+            other = lax.rem(half_at + step, pairs)
+            s1[step, taps] = (g1[2 * other + parity, taps].astype(F32) + r1[other, taps].astype(F32)).astype(BF16)
+            copy = remote(
+                s1.at[step, taps],
+                r2.at[step, taps],
+                r2_send.at[3 * step + a],
+                r2_recv.at[3 * step + a],
+                {"lat": 2 * other + parity},
+            )
+            copy.start()
+            second_stage.append(copy)
+
+    def run_third(a):
+        taps = pl.ds(3 * a, 3)
+        for step in range(1, pairs):
+            second_stage[a * (pairs - 1) + step - 1].wait_recv()
+        lat_sum = g1[2 * half_at + parity, taps].astype(F32) + r1[half_at, taps].astype(F32)
+        for step in range(1, pairs):
+            lat_sum = lat_sum + r2[step, taps].astype(F32)
+        for lon_at in range(nlon):
+            b3[lon_at, a] = jnp.concatenate(
+                [lat_sum[tap, lon_at * share : (lon_at + 1) * share] for tap in range(3)], axis=0
+            ).astype(BF16)
+        for step in range(1, nlon):
+            other = lax.rem(lo + step, nlon)
+            copy = remote(
+                b3.at[other, a], r3.at[step, a], r3_send.at[3 * step + a], r3_recv.at[3 * step + a], {"lon": other}
+            )
+            copy.start()
+            third_stage.append(copy)
+
+    def run_fourth(a):
+        for step in range(1, nlon):
+            third_stage[a * (nlon - 1) + step - 1].wait_recv()
+        lon_sum = b3[lo, a].astype(F32)
+        for step in range(1, nlon):
+            lon_sum = lon_sum + r3[step, a].astype(F32)
+        s4[dp, a] = lon_sum.astype(BF16)
+        for step in range(1, ndp):
+            copy = remote(
+                s4.at[dp, a],
+                s4.at[dp, a],
+                r4_send.at[3 * step - 3 + a],
+                r4_recv.at[3 * dp + a],
+                {"dp": lax.rem(dp + step, ndp)},
+            )
+            copy.start()
+            fourth_stage.append(copy)
+
+    if fast:
+        for a in range(3):
+            run_second(a)
 
     for row in range(rows):
         wide = gs[1, row + 1].astype(F32)
         gs[0, row + 1] = pltpu.roll(wide, 1, 0).astype(BF16)
         gs[2, row + 1] = pltpu.roll(wide, cols - 1, 0).astype(BF16)
-
-    second_stage = []
-    if fast:
-        for copy in first_stage:
-            copy.wait_recv()
-        for step in range(1, pairs):
-            other = lax.rem(half_at + step, pairs)
-            s1[step] = (g1[2 * other + parity].astype(F32) + r1[other].astype(F32)).astype(BF16)
-            second_stage.append(
-                remote(s1.at[step], r2.at[step], r2_send.at[step], r2_recv.at[step], {"lat": 2 * other + parity})
-            )
-            second_stage[-1].start()
 
     for at in range(8):
         guarded(g_copies[at][1], g_copies[at][2].wait_recv)
@@ -327,36 +387,16 @@
         small_dp_copies[-1].start()
 
     quarter = rows // 4
-    backward(0, quarter)
-    third_stage, fourth_stage = [], []
-    if fast:
-        share = own_lat // nlon
-        lat_sum = g1[2 * half_at + parity].astype(F32) + r1[half_at].astype(F32)
-        for copy in second_stage:
-            copy.wait_recv()
-        for step in range(1, pairs):
-            lat_sum = lat_sum + r2[step].astype(F32)
-        for lon_at in range(nlon):
-            b3[lon_at] = jnp.concatenate(
-                [lat_sum[tap, lon_at * share : (lon_at + 1) * share] for tap in range(9)], axis=0
-            ).astype(BF16)
-        for step in range(1, nlon):
-            other = lax.rem(lo + step, nlon)
-            third_stage.append(remote(b3.at[other], r3.at[step], r3_send.at[step], r3_recv.at[step], {"lon": other}))
-            third_stage[-1].start()
+    for a in range(3):
+        if fast:
+            run_third(a)
+        if a < 1:
+            backward(a * quarter, quarter)
     backward(quarter, quarter)
     backward(2 * quarter, quarter)
     if fast:
-        for copy in third_stage:
-            copy.wait_recv()
-        lon_sum = b3[lo].astype(F32)
-        for step in range(1, nlon):
-            lon_sum = lon_sum + r3[step].astype(F32)
-        s4[dp] = lon_sum.astype(BF16)
-        for step in range(1, ndp):
-            place = {"dp": lax.rem(dp + step, ndp)}
-            fourth_stage.append(remote(s4.at[dp], s4.at[dp], r4_send.at[step - 1], r4_recv.at[dp], place))
-            fourth_stage[-1].start()
+        for a in range(3):
+            run_fourth(a)
     backward(3 * quarter, quarter)
 
     cells = ndp * nlat * nlon * rows * cols
@@ -365,9 +405,16 @@
         other = lax.rem(dp + step, ndp)
         remote(small_dp.at[other], small_dp.at[other], sdp_send.at[step - 1], sdp_recv.at[other], {"dp": other}).wait_recv()
         if fast:
-            remote(s4.at[other], s4.at[other], r4_send.at[step - 1], r4_recv.at[other], {"dp": other}).wait_recv()
+            for a in range(3):
+                remote(
+                    s4.at[other, a], s4.at[other, a], r4_send.at[3 * step - 3 + a], r4_recv.at[3 * other + a], {"dp": other}
+                ).wait_recv()
     if fast:
-        gw_ref[...] = jnp.sum(s4[...].astype(F32), axis=0) * scale
+        for a in range(3):
+            part = s4[0, a].astype(F32)
+            for at in range(1, ndp):
+                part = part + s4[at, a].astype(F32)
+            gw_ref[3 * a * share : 3 * (a + 1) * share, :] = part * scale
     sum_ref[...] = jnp.sum(small_dp[...], axis=0) * scale
 
     for guard, _, copy in x_copies + g_copies:
@@ -403,6 +450,13 @@
         pltpu.VMEM((ndp, 2, chan), F32),
         dma(10), dma(10), dma(8), dma(8),
         dma(group), dma(group), dma(group), dma(group), dma(ndp), dma(ndp),
+        pltpu.VMEM(hidden_in.shape, BF16),
+        pltpu.VMEM((9 * chan, chan), BF16),
+        pltpu.VMEM((rows, cols), F32),
+        pltpu.VMEM((rows, cols), jnp.int32),
+        pltpu.VMEM((1, rows, cols), F32),
+        dma(5),
+        pltpu.VMEM((rows * cols, chan), F32),
     ]
     if fast:
         pairs = nlat // 2
@@ -411,24 +465,24 @@
             pltpu.VMEM((pairs, 9, own_lat, chan), BF16),
             pltpu.VMEM((pairs, 9, own_lat, chan), BF16),
             pltpu.VMEM((pairs, 9, own_lat, chan), BF16),
-            pltpu.VMEM((nlon, 9 * share, chan), BF16),
-            pltpu.VMEM((nlon, 9 * share, chan), BF16),
-            pltpu.VMEM((ndp, 9 * share, chan), BF16),
-            dma(3 * pairs), dma(3 * pairs), dma(pairs), dma(pairs), dma(nlon), dma(nlon), dma(ndp), dma(ndp),
+            pltpu.VMEM((nlon, 3, 3 * share, chan), BF16),
+            pltpu.VMEM((nlon, 3, 3 * share, chan), BF16),
+            pltpu.VMEM((ndp, 3, 3 * share, chan), BF16),
+            dma(3 * pairs), dma(3 * pairs), dma(3 * pairs), dma(3 * pairs), dma(3 * nlon), dma(3 * nlon), dma(3 * ndp), dma(3 * ndp),
         ]
-    vmem, smem = pl.BlockSpec(memory_space=pltpu.VMEM), pl.BlockSpec(memory_space=pltpu.SMEM)
+    vmem, smem, hbm = (pl.BlockSpec(memory_space=space) for space in (pltpu.VMEM, pltpu.SMEM, pltpu.HBM))
     gw_shape = (9 * share, chan) if fast else (9, chan, chan)
     grad_hidden, weight_part, sums = pl.pallas_call(
         functools.partial(kernel, dims),
         out_shape=(
-            jax.ShapeDtypeStruct(hidden_in.shape, BF16),
-            jax.ShapeDtypeStruct(gw_shape, F32),
-            jax.ShapeDtypeStruct((2, chan), F32),
+            pltpu.VMEM(hidden_in.shape, BF16),
+            pltpu.VMEM(gw_shape, F32),
+            pltpu.VMEM((2, chan), F32),
         ),
-        in_specs=[vmem] * 6 + [smem] * 2 + [vmem],
+        in_specs=[hbm, hbm, vmem, vmem, hbm, hbm, smem, smem, hbm],
         out_specs=(vmem, vmem, vmem),
         scratch_shapes=scratch,
-        compiler_params=pltpu.CompilerParams(collective_id=0, has_side_effects=True, vmem_limit_bytes=48 * 1024 * 1024),
+        compiler_params=pltpu.CompilerParams(collective_id=0, has_side_effects=True, vmem_limit_bytes=(66403328 if fast else 48 * 1024 * 1024)),
     )(
         hidden_in,
         conv_weight.reshape(9 * chan, chan),

time: 35.6 us -> 29.9 us (0.84)
  local copies, waits for them, and re-layouts: 6.69 us -> 1.93 us
  Pallas kernels: 27.9 us -> 27.1 us
    unnamed x20 -> x2, local copies, waits for them, and re-layouts: 6.17 us -> 1.41 us
    pallas_call x1, Pallas kernels: 27.9 us -> 27.1 us  [shards(): pl.pallas_call(functools.partial(kernel, dims), out_shape=(pltpu.VMEM(hid...]
where the time goes in v2:
time: 29.9 us; the launch traced here: 29.7 us
  Pallas kernels  27.1 us (91%)
  local copies, waits for them, and re-layouts  1.93 us (6%)
  between operations  0.64 us (2%)
    pallas_call x1, Pallas kernels, shards(): pl.pallas_call(functools.partial(kernel, dims), out_shape=(pltpu.VMEM(hid...  27.1 us
    unnamed x2, local copies, waits for them, and re-layouts  1.41 us

profile of v2, /device:TPU:0, one launch (start us, length us, event | category | flops | bytes accessed | tf_op | source)
XLA Modules:
  0.0 29.7 jit_solution(5375281565090795447)
XLA Ops:
  0.6 27.1 %shard_map.120 = (bf16[1,16,128,128]{3,2,1,0:T(8,128)(2,1)S(1)}, f32[72,128]{1,0:T(8,128)S(1)}, f32[2,128]{1,0:T(2,128)S(1)}) custom-call(bf16[1,16,128,128]{3,2,1,0:T(8,128)(2,1)} %refs_0_.1, bf16[1152,128]{1,0:T(8,128)(2,1)} %bitcast.11, f32[1,128]{1,0:T(1,128)} %bitcast.12, f32[1,128]{1,0:T(1,128)} %bitcast.13, f32[16,128]{1,0:T(8,128)} %refs_4_.1, ...), custom_call_target="tpu_custom_call" | custom-call | tf_op jit(solution)/shard_map/pallas_call | solution.py:475
  27.8 0.8 %copy.15 = bf16[1,16,128,128]{3,2,1,0:T(8,128)(2,1)} copy(bf16[1,16,128,128]{3,2,1,0:T(8,128)(2,1)S(1)} %get-tuple-element.12) | data formatting | bytes 1048576
  28.6 0.6 %copy.16 = f32[8,3,3,128]{3,0,2,1:T(8,128)} copy(f32[8,3,3,128]{3,0,2,1:T(8,128)S(1)} %bitcast.10) | data formatting | bytes 73728
  29.2 0.5 %slice_bitcast_fusion = (f32[128]{0:T(128)}, f32[128]{0:T(128)}) fusion(f32[2,128]{1,0:T(2,128)S(1)} %get-tuple-element.9), kind=kLoop, calls=%fused_computation | loop fusion | bytes 2048 | tf_op jit(solution)/shard_map/squeeze | solution.py:503
